TPU v7x, 128 devices: a whole 4x4x4 slice. The times are simulated.
128 devices in a mesh: row: 8 (over z, core), col: 16 (over x, y).
Axes of the slice: x: 4, y: 4, z: 4, core: 2. Of those that a mesh axis runs over, the one named last changes fastest.
Arguments:
- trial_factor: bfloat16 [2, 8192, 512], P(None, ('row', 'col')), may hold values from -6 to 6
- occupied: bfloat16 [8192, 512], P(('col', 'row')), may hold values from -0.25 to 0.25
- centers: float32 [3, 8192], P(None, ('row', 'col')), may hold values from 0 to 1
- exponents: float32 [8192], P(('row', 'col')), may hold values from 0.5 to 4
- wave_vectors: float32 [3, 8192], P(None, ('row', 'col')), may hold values from -36 to 36
- phases: float32 [8192], P(('row', 'col')), may hold values from -3.140625 to 3.140625
- points: float32 [256, 3, 1024], P(('row', 'col')), may hold values from 0 to 1
- density: float32 [256, 1024], P(('row', 'col')), may hold values from 0.05 to 1
- weights: float32 [256, 1024], P(('row', 'col')), may hold values from 0.0001 to 0.001
- sources: int32 [256, 8, 1], P(('row', 'col')), may hold values from 0 to 15; in each aligned block of 16 rows (0 to 15, 16 to 31, ..., all dimensions but the last counted through in order) at most 2 rows name the same one
Outputs:
- response: float32 [8192, 2, 512], P(('row', 'col'))
Inputs may be any that keep to these rules, and one draw needn't show every extreme that they name: `sources`: among the 16 entries of the batches of one device, no column block is named more than 2 times, and some block exactly 2 times.
All inputs are finite; a program needn't handle non-finite values.
Results may differ from a plain program's by a relative error of at most 0.0065.
Values may be sent and summed in bfloat16 or wider, within the bound.
A program may use at most 128 MiB of HBM per device.

v0:
```python
import jax
import jax.numpy as jnp
from jax import lax
from jax.sharding import PartitionSpec as P

TB = 256
EXCHANGE_COEF = 0.75 * (3.0 / 3.141592653589793) ** (1.0 / 3.0)


def rows_first(arrays, axis, dims):
    turned = [jnp.moveaxis(a, dim, 0) for a, dim in zip(arrays, dims)]
    both = jnp.concatenate([t.reshape(len(t), -1) for t in turned], axis=1)
    filled, at, finished = (lax.all_gather(both, axis, axis=0, tiled=True), 0, [])
    for t, dim in zip(turned, dims):
        slab = filled[:, at : at + t[0].size].reshape(-1, *t.shape[1:])
        finished.append(jnp.moveaxis(slab, 0, dim))
        at += t[0].size
    return tuple(finished)


def joined_along(tiles, dim):
    tiles = jnp.moveaxis(tiles, 0, dim)
    shape = tiles.shape
    return tiles.reshape(*shape[:dim], shape[dim] * shape[dim + 1], *shape[dim + 2 :])


def sent_to_all(value, axis):
    size = lax.axis_size(axis)
    return lax.all_to_all(
        jnp.broadcast_to(value[None], (size, *value.shape)), axis, 0, 0, tiled=True
    )


def gather_directly(value, axis, dim):
    return joined_along(sent_to_all(value, axis), dim)


def split_up(value, dim, size):
    shape = value.shape
    tiles = value.reshape(*shape[:dim], size, shape[dim] // size, *shape[dim + 1 :])
    return jnp.moveaxis(tiles, dim, 0)


def sum_at_owner(value, axis, dim):
    size = lax.axis_size(axis)
    tiles = lax.all_to_all(split_up(value, dim, size), axis, 0, 0, tiled=True)
    return jnp.sum(tiles.astype(jnp.float32), axis=0)


def collocate(grid_points, func_centers, func_exponents, func_waves, func_phases):
    npoints = grid_points.shape[1]
    nfuncs = func_centers.shape[1]
    radius = jnp.zeros((npoints, nfuncs), jnp.float32)
    phase_sum = jnp.zeros((npoints, nfuncs), jnp.float32) + func_phases[None, :]
    for coordinate in range(3):
        offset = grid_points[coordinate][:, None] - func_centers[coordinate][None, :]
        radius = radius + offset * offset
        phase_sum = phase_sum + grid_points[coordinate][:, None] * func_waves[coordinate][None, :]
    return (jnp.exp(-func_exponents[None, :] * radius) * jnp.cos(phase_sum)).astype(jnp.bfloat16)


def batch_response(ground, quad_weights, row_values, col_values, pair_tiles):
    npoints = col_values.shape[0]
    row_tiles = pair_tiles.shape[0]
    col_span = pair_tiles.shape[1]
    tile_width = pair_tiles.shape[2]
    tile_size = row_values.shape[1] // row_tiles
    vectors = tile_width // tile_size
    col_phi = col_values.reshape(npoints, row_tiles, col_span)
    half_contracted = jnp.einsum(
        "gax,axy->gay", col_phi, pair_tiles, preferred_element_type=jnp.float32
    )
    half_contracted = half_contracted.reshape(npoints, row_tiles, vectors, tile_size)
    row_phi = row_values.astype(jnp.float32).reshape(npoints, row_tiles, 1, tile_size)
    response_density = jnp.sum(half_contracted * row_phi, axis=(1, 3))
    kernel = -(4.0 / 9.0) * EXCHANGE_COEF * jnp.exp(-(2.0 / 3.0) * jnp.log(ground))
    potential = (quad_weights * kernel)[:, None] * response_density
    scaled = (
        (potential[:, None, :, None] * row_phi)
        .astype(jnp.bfloat16)
        .reshape(npoints, row_tiles, tile_width)
    )
    matrix = jnp.einsum("gax,gay->axy", col_phi, scaled, preferred_element_type=jnp.float32)
    return matrix.astype(jnp.bfloat16)


def per_device(
    trial_factor,
    occupied,
    centers,
    exponents,
    wave_vectors,
    phases,
    points,
    density,
    weights,
    sources,
):
    columns = lax.axis_size("col")
    row_block = lax.axis_index("row")
    all_centers, all_waves, all_exponents, all_phases = rows_first(
        (centers, wave_vectors, exponents, phases), ("row", "col"), (1, 1, 0, 0)
    )
    col_factor = gather_directly(occupied, "row", 0)
    span_col = col_factor.shape[0]
    orbital_count = col_factor.shape[1]
    tiles_col = span_col // TB
    span_row = trial_factor.shape[1] * columns
    tiles_row = span_row // TB
    vectors = trial_factor.shape[0]
    pair_count = tiles_row * tiles_col
    batch_count = sources.shape[0]
    slot_count = batch_count * pair_count
    slot_source = sources.reshape(slot_count)
    capacity = max(2, (slot_count + columns - 1) // columns)
    source_hot = (slot_source[:, None] == jnp.arange(columns, dtype=jnp.int32)[None, :]).astype(
        jnp.int32
    )
    slot_rank = jnp.sum(source_hot * (jnp.cumsum(source_hot, axis=0) - 1), axis=1)
    slot_place = slot_source * capacity + slot_rank
    slot_pair = jnp.arange(slot_count, dtype=jnp.int32) % pair_count
    place_hot = slot_place[:, None] == jnp.arange(columns * capacity, dtype=jnp.int32)[None, :]
    place_matrix = place_hot.astype(jnp.bfloat16)
    wanted = jnp.sum(place_hot.astype(jnp.int32) * (slot_pair[:, None] + 1), axis=0) - 1
    asked_pairs = lax.all_to_all(
        wanted.reshape(columns, capacity), "col", split_axis=0, concat_axis=0, tiled=True
    )
    asked_flat = asked_pairs.reshape(columns * capacity)
    asked_col = jnp.where(asked_flat >= 0, asked_flat % tiles_col, -1)
    col_hot = (asked_col[:, None] == jnp.arange(tiles_col, dtype=jnp.int32)[None, :]).astype(
        jnp.bfloat16
    )
    row_start = row_block * span_row
    row_centers = lax.dynamic_slice_in_dim(all_centers, row_start, span_row, 1)
    row_waves = lax.dynamic_slice_in_dim(all_waves, row_start, span_row, 1)
    row_exponents = lax.dynamic_slice_in_dim(all_exponents, row_start, span_row, 0)
    row_phases = lax.dynamic_slice_in_dim(all_phases, row_start, span_row, 0)
    tile_offsets = jnp.arange(TB, dtype=jnp.int32)
    column_tile = slot_source * tiles_col + slot_pair % tiles_col
    column_index = (column_tile[:, None] * TB + tile_offsets[None, :]).reshape(
        batch_count, pair_count * TB
    )
    row_trial = gather_directly(trial_factor, "col", 1)
    row_split = row_trial.reshape(vectors, tiles_row, TB, orbital_count)
    outgoing_rows = (
        jnp.dot(
            col_hot,
            col_factor.reshape(tiles_col, TB * orbital_count),
            preferred_element_type=jnp.float32,
        )
        .astype(jnp.bfloat16)
        .reshape(columns, capacity, TB * orbital_count)
    )
    incoming_rows = lax.all_to_all(outgoing_rows, "col", split_axis=0, concat_axis=0, tiled=True)
    slot_rows = jnp.dot(
        place_matrix,
        incoming_rows.reshape(columns * capacity, TB * orbital_count),
        preferred_element_type=jnp.float32,
    ).astype(jnp.bfloat16)
    slot_rows = slot_rows.reshape(batch_count, tiles_row, tiles_col * TB, orbital_count)
    accumulated = jnp.zeros((span_row, vectors, orbital_count), jnp.float32)
    for position in range(batch_count):
        factor_rows = slot_rows[position]
        tiles_now = (
            jnp.einsum("kami,axi->axkm", row_split, factor_rows, preferred_element_type=jnp.float32)
            .astype(jnp.bfloat16)
            .reshape(tiles_row, tiles_col * TB, vectors * TB)
        )
        index_now = column_index[position]
        row_values = collocate(points[position], row_centers, row_exponents, row_waves, row_phases)
        col_values = collocate(
            points[position],
            jnp.take(all_centers, index_now, axis=1),
            jnp.take(all_exponents, index_now),
            jnp.take(all_waves, index_now, axis=1),
            jnp.take(all_phases, index_now),
        )
        potential_now = batch_response(
            density[position], weights[position], row_values, col_values, tiles_now
        )
        contrib = jnp.einsum(
            "axkm,axi->amki",
            potential_now.reshape(tiles_row, tiles_col * TB, vectors, TB),
            factor_rows,
            preferred_element_type=jnp.float32,
        )
        accumulated = accumulated + contrib.reshape(span_row, vectors, orbital_count)
    return sum_at_owner(accumulated.astype(jnp.bfloat16), "col", 0)


def solution(mesh):
    in_specs = (
        P(None, ("row", "col"), None),
        P(("col", "row"), None),
        P(None, ("row", "col")),
        P(("row", "col")),
        P(None, ("row", "col")),
        P(("row", "col")),
        P(("row", "col"), None, None),
        P(("row", "col"), None),
        P(("row", "col"), None),
        P(("row", "col"), None, None),
    )
    out_specs = P(("row", "col"), None, None)
    return jax.shard_map(
        per_device, mesh=mesh, in_specs=in_specs, out_specs=out_specs, check_vma=False
    )
```

profile of v0, /device:TPU:0, one launch (start us, length us, event | category | flops | bytes accessed | tf_op | source)
XLA Modules:
  0.0 501.2 jit_solution(6194793369204841043)
XLA Ops:
  0.5 1.3 reduce.54
  2.4 14.6 %all_to_all.26 = s32[16,1,2]{2,1,0:T(1,128)S(1)} all-to-all(s32[16,1,2]{2,1,0:T(1,128)S(1)} %bitcast.131), channel_id=1, replica_groups=mesh['row'=8,'col'=16] {'col'}, dimensions={0} | all-to-all | bytes 256 | tf_op jit(solution)/shard_map/all_to_all | solution.py:125
  17.9 15.5 %all_to_all.27 = bf16[8,64,512]{2,1,0:T(8,128)(2,1)S(1)} all-to-all(bf16[8,64,512]{2,1,0:T(8,128)(2,1)S(1)} %broadcast_in_dim.16), channel_id=1, replica_groups=mesh['row'=8,'col'=16] {'row'}, dimensions={0} | all-to-all | bytes 1048576 | tf_op jit(solution)/shard_map/all_to_all | solution.py:29
  33.3 2.5 broadcast_in_dim.17
  35.8 3.7 all-to-all-start.3
  39.7 73.3 %all-gather = f32[128,64,8]{1,2,0:T(8,128)S(1)} all-gather(f32[1,64,8]{1,2,0:T(8,128)S(1)} %maximum_bitcast_fusion), channel_id=1, replica_groups=mesh['row'=8,'col'=16] {'row','col'}, dimensions={0}, use_global_device_ids=true | all-gather | bytes 264192 | tf_op jit(solution)/shard_map/all_gather | solution.py:13
  113.0 2.6 copy.26
  116.8 5.6 %convolution_convert_fusion = bf16[32,131072]{1,0:T(8,128)(2,1)} fusion(bf16[2,131072]{1,0:T(2,128)(2,1)S(1)} %reshape_reshape.6, s32[32]{0:T(128)S(1)} %compare_select_fusion.6), kind=kOutput, calls=%fused_computation.8 | convolution fusion | flops 20971584 | bytes 8913024 | tf_op jit(solution)/shard_map/dot_general | solution.py:146
  122.4 9.4 %reshape.626 = bf16[16,2,131072]{2,1,0:T(2,128)(2,1)} reshape(bf16[32,131072]{1,0:T(8,128)(2,1)} %convolution_convert_fusion) | data formatting | bytes 16777216 | tf_op jit(solution)/shard_map/reshape | solution.py:152
  131.7 1.4 copy-done.3
  133.1 5.3 %all-to-all-start.2 = ((bf16[16,2,131072]{2,1,0:T(2,128)(2,1)}), bf16[16,2,131072]{2,1,0:T(2,128)(2,1)}, u32[]{:S(2)}, u32[]{:S(2)}) async-start(bf16[16,2,131072]{2,1,0:T(2,128)(2,1)} %reshape.626), calls=%async_computation.2 | async-start | bytes 16777216 | tf_op jit(solution)/shard_map/all_to_all | solution.py:154
  138.4 9.0 %slice_reduce_fusion.19 = (f32[8192]{0:T(1024)S(1)}, f32[8192]{0:T(1024)S(1)}, f32[8192,1]{1,0:T(8,128)}, f32[8192,1]{1,0:T(8,128)}) fusion(f32[8192,8]{1,0:T(8,128)} %bitcast.98), kind=kLoop, calls=%fused_computation.112 | loop fusion | bytes 196608 | tf_op jit(solution)/shard_map/slice | solution.py:15
  147.3 11.8 %gather_fusion.4 = f32[2048]{0:T(1024)S(1)} fusion(f32[8192]{0:T(1024)S(1)} %get-tuple-element.6, s32[2048]{0:T(1024)S(1)} %fusion.27), kind=kCustom, calls=%fused_computation.3.clone | custom fusion | bytes 24576 | tf_op jit(solution)/shard_map/jit(_take)/gather | solution.py:174
  159.1 11.8 %gather_fusion = f32[2048]{0:T(1024)S(1)} fusion(f32[8192]{0:T(1024)S(1)} %get-tuple-element.6, s32[2048]{0:T(1024)S(1)} %fusion.26), kind=kCustom, calls=%fused_computation.clone | custom fusion | bytes 24576 | tf_op jit(solution)/shard_map/jit(_take)/gather | solution.py:174
  170.9 11.8 %gather_fusion.6 = f32[2048]{0:T(1024)S(1)} fusion(f32[8192]{0:T(1024)S(1)} %get-tuple-element.8, s32[2048]{0:T(1024)S(1)} %fusion.27), kind=kCustom, calls=%fused_computation.4.clone | custom fusion | bytes 24576 | tf_op jit(solution)/shard_map/jit(_take)/gather | solution.py:176
  182.7 11.8 %gather_fusion.2 = f32[2048]{0:T(1024)S(1)} fusion(f32[8192]{0:T(1024)S(1)} %get-tuple-element.8, s32[2048]{0:T(1024)S(1)} %fusion.26), kind=kCustom, calls=%fused_computation.2.clone | custom fusion | bytes 24576 | tf_op jit(solution)/shard_map/jit(_take)/gather | solution.py:176
  194.5 10.6 %slice_bitcast_fusion.3 = (f32[3,8192]{0,1:T(8,128)}, f32[3,8192]{0,1:T(8,128)}, f32[8192,3]{1,0:T(8,128)}, f32[8192,3]{1,0:T(8,128)}) fusion(f32[8192,8]{1,0:T(8,128)} %bitcast.99), kind=kLoop, calls=%fused_computation.111 | loop fusion | bytes 589824 | tf_op jit(solution)/shard_map/transpose | solution.py:16
  205.1 7.6 %gather_fusion.5 = f32[2048,3]{1,0:T(8,128)S(1)} fusion(f32[3,8192]{0,1:T(8,128)} %get-tuple-element.33, s32[2048]{0:T(1024)S(1)} %fusion.27), kind=kCustom, calls=%fused_computation.6.clone | custom fusion | bytes 57344 | tf_op jit(solution)/shard_map/jit(_take)/gather | solution.py:173
  212.7 7.6 %gather_fusion.1 = f32[2048,3]{1,0:T(8,128)S(1)} fusion(f32[3,8192]{0,1:T(8,128)} %get-tuple-element.33, s32[2048]{0:T(1024)S(1)} %fusion.26), kind=kCustom, calls=%fused_computation.1.clone | custom fusion | bytes 57344 | tf_op jit(solution)/shard_map/jit(_take)/gather | solution.py:173
  220.4 9.8 %gather_fusion.3 = f32[2048,3]{1,0:T(8,128)} fusion(f32[3,8192]{0,1:T(8,128)} %get-tuple-element.34, s32[2048]{0:T(1024)S(1)} %fusion.26), kind=kCustom, calls=%fused_computation.5.clone | custom fusion | bytes 57344 | tf_op jit(solution)/shard_map/jit(_take)/gather | solution.py:175
  230.1 9.9 %gather_fusion.7 = f32[2048,3]{1,0:T(8,128)} fusion(f32[3,8192]{0,1:T(8,128)} %get-tuple-element.34, s32[2048]{0:T(1024)S(1)} %fusion.27), kind=kCustom, calls=%fused_computation.7.clone | custom fusion | bytes 57344 | tf_op jit(solution)/shard_map/jit(_take)/gather | solution.py:175
  240.0 1.5 dynamic-slice_reduce_fusion
  241.7 1.3 dynamic-slice_bitcast_fusion
  244.6 1.6 select_bitcast_fusion.3
  246.2 1.4 slice_reduce_fusion.11
  247.7 1.6 select_bitcast_fusion.1
  249.3 1.4 slice_reduce_fusion.5
  250.8 1.4 slice_reduce_fusion.2
  252.3 1.4 slice_reduce_fusion.8
  253.9 33.1 %fusion.5 = (f32[1024,4,256]{0,2,1:T(8,128)}, f32[1024,4,256]{0,2,1:T(8,128)}) fusion(f32[1024]{0:T(1024)S(1)} %bitcast.116, f32[1024]{0:T(1024)S(1)} %bitcast.119, f32[1024]{0:T(1024)S(1)} %bitcast.113, f32[4,256]{1,0:T(4,128)S(1)} %mul.505, f32[4,256]{1,0:T(4,128)S(1)} %mul.502, f32[4,256]{1,0:T(4,128)S(1)} %mul.499, f32[4,256]{1,0:T(4,128)S(1)} %add.256, ...), kind=kLoop, calls=%fused_computation.25 | loop fusion | flops 37748736 | bytes 8445952 | tf_op jit(solution)/shard_map/convert_element_type | solution.py:74
  286.9 1.6 copy.27
  288.6 8.6 %reshape.627 = bf16[32,131072]{1,0:T(8,128)(2,1)} reshape(bf16[16,2,131072]{2,1,0:T(2,128)(2,1)} %all-to-all-done.2) | data formatting | bytes 16777216 | tf_op jit(solution)/shard_map/reshape | solution.py:157
  297.2 4.7 convolution_convert_fusion.1
  301.9 1.6 fusion.33
  303.5 2.2 reshape.729
  305.8 2.5 reshape.728
  308.3 3.0 fusion.13
  311.4 1.3 fusion.16
  313.6 33.8 %fusion.2 = f32[1024,512]{0,1:T(8,128)S(1)} fusion(f32[1024,4,256]{0,2,1:T(8,128)S(1)} %copy-done, bf16[4,512,512]{1,2,0:T(8,128)(2,1)S(1)} %bitcast.106, f32[4,512]{1,0:T(4,128)S(1)} %mul.529, f32[4,512]{1,0:T(4,128)S(1)} %mul.526, f32[4,512]{1,0:T(4,128)S(1)} %mul.523, f32[4,512]{1,0:T(4,128)S(1)} %add.263, f32[4,512]{1,0:T(4,128)S(1)} %sub.262, ...), kind=kOutput, calls=%fused_computation.16 | convolution fusion | flops 2186805248 | bytes 8466432 | tf_op jit(solution)/shard_map/gax,axy->gay/dot_general | solution.py:70
  347.6 33.6 %fusion = f32[1024,512]{0,1:T(8,128)S(1)} fusion(f32[1024,4,256]{0,2,1:T(8,128)S(1)} %copy-done.1, bf16[4,512,512]{1,2,0:T(8,128)(2,1)S(1)} %bitcast.105, f32[4,512]{1,0:T(4,128)S(1)} %mul.484, f32[4,512]{1,0:T(4,128)S(1)} %mul.481, f32[4,512]{1,0:T(4,128)S(1)} %mul.478, f32[4,512]{1,0:T(4,128)S(1)} %add.248, f32[4,512]{1,0:T(4,128)S(1)} %sub.235, ...), kind=kOutput, calls=%fused_computation.14 | convolution fusion | flops 2186805248 | bytes 8466432 | tf_op jit(solution)/shard_map/gax,axy->gay/dot_general | solution.py:70
  381.6 1.6 fusion.1
  383.2 33.7 %convolution_convert_fusion.3 = bf16[4,512,512]{1,2,0:T(8,128)(2,1)S(1)} fusion(bf16[1024,4,512]{0,2,1:T(8,128)(2,1)S(1)} %fusion.1, f32[4,512]{1,0:T(4,128)S(1)} %mul.484, f32[4,512]{1,0:T(4,128)S(1)} %mul.481, f32[4,512]{1,0:T(4,128)S(1)} %mul.478, f32[4,512]{1,0:T(4,128)S(1)} %add.248, f32[4,512]{1,0:T(4,128)S(1)} %sub.235, f32[1024]{0:T(1024)S(1)} %bitcast.124, ...), kind=kOutput, calls=%fused_computation.38 | convolution fusion | flops 2184183808 | bytes 6369280 | tf_op jit(solution)/shard_map/gax,gay->axy/dot_general | solution.py:83
  416.9 1.2 fusion.9
  418.5 1.6 fusion.3
  420.0 42.9 %convolution_convert_fusion.2 = bf16[4,512,512]{1,2,0:T(8,128)(2,1)S(1)} fusion(bf16[1024,4,512]{0,2,1:T(8,128)(2,1)S(1)} %fusion.3, f32[4,512]{1,0:T(4,128)S(1)} %mul.529, f32[4,512]{1,0:T(4,128)S(1)} %mul.526, f32[4,512]{1,0:T(4,128)S(1)} %mul.523, f32[4,512]{1,0:T(4,128)S(1)} %add.263, f32[4,512]{1,0:T(4,128)S(1)} %sub.262, f32[1024]{0:T(1024)S(1)} %bitcast.118, ...), kind=kOutput, calls=%fused_computation.37 | convolution fusion | flops 2184183808 | bytes 6369280 | tf_op jit(solution)/shard_map/gax,gay->axy/dot_general | solution.py:83
  463.0 1.3 fusion.21
  464.7 35.1 %all_to_all.28 = bf16[16,64,2,512]{3,1,2,0:T(8,128)(2,1)S(1)} all-to-all(bf16[16,64,2,512]{3,1,2,0:T(8,128)(2,1)S(1)} %copy.31), channel_id=1, replica_groups=mesh['row'=8,'col'=16] {'col'}, dimensions={0} | all-to-all | bytes 4194304 | tf_op jit(solution)/shard_map/all_to_all | solution.py:46
  500.1 0.9 copy.33
  (89 shorter events, 7.5 us)
Async XLA Ops:
  0.0 39.6 %copy-start.11 = (f32[64]{0:T(128)S(1)}, f32[64]{0:T(128)}, u32[]{:S(2)}) copy-start(f32[64]{0:T(128)} %param.19) | copy-start | bytes 772
  0.0 39.6 %copy-start.9 = (f32[3,64]{1,0:T(4,128)S(1)}, f32[3,64]{1,0:T(4,128)}, u32[]{:S(2)}) copy-start(f32[3,64]{1,0:T(4,128)} %param.18) | copy-start | bytes 2308
  0.0 39.6 %copy-start.12 = (f32[64]{0:T(128)S(1)}, f32[64]{0:T(128)}, u32[]{:S(2)}) copy-start(f32[64]{0:T(128)} %param.17) | copy-start | bytes 772
  0.0 39.7 %copy-start.10 = (f32[3,64]{1,0:T(4,128)S(1)}, f32[3,64]{1,0:T(4,128)}, u32[]{:S(2)}) copy-start(f32[3,64]{1,0:T(4,128)} %param.16) | copy-start | bytes 2308
  35.8 95.9 %all-to-all-start.3 = ((bf16[16,2,64,512]{3,2,1,0:T(8,128)(2,1)}), bf16[16,2,64,512]{3,2,1,0:T(8,128)(2,1)S(1)}, u32[]{:S(2)}, u32[]{:S(2)}) async-start(bf16[16,2,64,512]{3,2,1,0:T(8,128)(2,1)} %broadcast_in_dim.17), calls=%async_computation.3 | async-start | bytes 4194304 | tf_op jit(solution)/shard_map/all_to_all | solution.py:29
  131.7 1.4 copy-start.3
  133.1 155.5 %all-to-all-start.2 = ((bf16[16,2,131072]{2,1,0:T(2,128)(2,1)}), bf16[16,2,131072]{2,1,0:T(2,128)(2,1)}, u32[]{:S(2)}, u32[]{:S(2)}) async-start(bf16[16,2,131072]{2,1,0:T(2,128)(2,1)} %reshape.626), calls=%async_computation.2 | async-start | bytes 16777216 | tf_op jit(solution)/shard_map/all_to_all | solution.py:154
  249.2 4.5 copy-start.7
  249.2 4.5 copy-start.8
  249.3 4.6 copy-start.6
  253.8 33.1 %copy-start.4 = (bf16[16,2,64,512]{3,2,1,0:T(8,128)(2,1)S(1)}, bf16[16,2,64,512]{3,2,1,0:T(8,128)(2,1)}, u32[]{:S(2)}) copy-start(bf16[16,2,64,512]{3,2,1,0:T(8,128)(2,1)} %copy-done.3) | copy-start | bytes 6291460
  308.3 3.1 copy-start.2
  308.3 3.1 copy-start.5
  311.4 2.2 copy-start
  313.6 34.0 %copy-start.1 = (f32[1024,4,256]{0,2,1:T(8,128)S(1)}, f32[1024,4,256]{0,2,1:T(8,128)}, u32[]{:S(2)}) copy-start(f32[1024,4,256]{0,2,1:T(8,128)} %get-tuple-element.40) | copy-start | bytes 12582916
where the time goes:
time: 507 us; the launch traced here: 501 us
  matrix products  161 us (32%)
  local copies, waits for them, and re-layouts  148 us (29%)
  blocking collectives  138 us (27%)
  other arithmetic  44 us (9%)
  starting transfers between devices  8.98 us (2%)
    dot_general x2, matrix products, batch_response(): jnp.einsum('gax,gay->axy', col_phi, scaled, preferred_element_type=jnp.fl...  76.7 us
    all_gather x1, blocking collectives, rows_first(): lax.all_gather(both, axis, axis=0, tiled=True)  73.3 us
    dot_general x2, matrix products, batch_response(): jnp.einsum('gax,axy->gay', col_phi, pair_tiles, preferred_element_type=jn...  67.5 us
    all_to_all x1, blocking collectives, sum_at_owner(): tiles = lax.all_to_all(split_up(value, dim, size), axis, 0, 0, tiled=True)  35.1 us
    convert_element_type x1, other arithmetic, batch_response(): row_values.astype(jnp.float32).reshape(npoints, row_tiles, 1, tile_size)  33.1 us
    gather x2, local copies, waits for them, and re-layouts, per_device(): jnp.take(all_phases, index_now)  23.6 us
    gather x2, local copies, waits for them, and re-layouts, per_device(): jnp.take(all_exponents, index_now)  23.6 us
    gather x2, local copies, waits for them, and re-layouts, per_device(): jnp.take(all_waves, index_now, axis=1)  19.6 us
  transfers between devices with their start and end apart: 2, of which 0 were waited for; matrix products, arithmetic and copies ran while one was open for 34% of the time, Pallas kernels for 0%

commit v1 on v0

--- a/solution.py
+++ b/solution.py
@@ -10,7 +10,13 @@
 def rows_first(arrays, axis, dims):
     turned = [jnp.moveaxis(a, dim, 0) for a, dim in zip(arrays, dims)]
     both = jnp.concatenate([t.reshape(len(t), -1) for t in turned], axis=1)
-    filled, at, finished = (lax.all_gather(both, axis, axis=0, tiled=True), 0, [])
+    filled, at, finished = (
+        jnp.concatenate(
+            lax.all_to_all(jnp.stack([both] * lax.axis_size(axis)), axis, 0, 0), axis=0
+        ),
+        0,
+        [],
+    )
     for t, dim in zip(turned, dims):
         slab = filled[:, at : at + t[0].size].reshape(-1, *t.shape[1:])
         finished.append(jnp.moveaxis(slab, 0, dim))

time: 507 us -> 463 us (0.913)
  blocking collectives: 138 us -> 62.9 us
  waiting for transfers between devices: 0.01 us -> 20.3 us
  starting transfers between devices: 8.98 us -> 16.1 us
    all_gather x1 -> x0, blocking collectives: 73.3 us -> none  [rows_first(): lax.all_gather(both, axis, axis=0, tiled=True)]
    all_to_all x1, waiting for transfers between devices: 0.01 us -> 13.9 us  [sent_to_all(): lax.all_to_all(jnp.broadcast_to(value[None], (size, *value.shape)), axis,...]
    all_to_all x0 -> x1, starting transfers between devices: none -> 7.15 us  [per_device(): lax.all_to_all(wanted.reshape(columns, capacity), 'col', split_axis=0, co...]
    all_to_all x0 -> x1, waiting for transfers between devices: none -> 6.4 us  [per_device(): lax.all_to_all(wanted.reshape(columns, capacity), 'col', split_axis=0, co...]
  transfers between devices with their start and end apart: 2 -> 3, of which waited for: 0 -> 2; matrix products, arithmetic and copies ran while one was open for 34% -> 38% of each run, Pallas kernels for 0% -> 0%
where the time goes in v1:
time: 463 us; the launch traced here: 457 us
  matrix products  161 us (35%)
  local copies, waits for them, and re-layouts  149 us (32%)
  blocking collectives  62.9 us (14%)
  other arithmetic  46.1 us (10%)
  waiting for transfers between devices  20.3 us (4%)
  starting transfers between devices  16.1 us (3%)
    dot_general x2, matrix products, batch_response(): jnp.einsum('gax,gay->axy', col_phi, scaled, preferred_element_type=jnp.fl...  76.7 us
    dot_general x2, matrix products, batch_response(): jnp.einsum('gax,axy->gay', col_phi, pair_tiles, preferred_element_type=jn...  67.5 us
    convert_element_type x1, other arithmetic, batch_response(): row_values.astype(jnp.float32).reshape(npoints, row_tiles, 1, tile_size)  33.1 us
    all_to_all x1, blocking collectives, sum_at_owner(): tiles = lax.all_to_all(split_up(value, dim, size), axis, 0, 0, tiled=True)  32.2 us
    gather x2, local copies, waits for them, and re-layouts, per_device(): jnp.take(all_phases, index_now)  23.6 us
    gather x2, local copies, waits for them, and re-layouts, per_device(): jnp.take(all_exponents, index_now)  23.6 us
    gather x2, local copies, waits for them, and re-layouts, per_device(): jnp.take(all_waves, index_now, axis=1)  19.6 us
    all_to_all x1, blocking collectives, rows_first(): lax.all_to_all(jnp.stack([both] * lax.axis_size(axis)), axis, 0, 0)  17.9 us
  transfers between devices with their start and end apart: 3, of which 2 were waited for; matrix products, arithmetic and copies ran while one was open for 38% of the time, Pallas kernels for 0%

profile of v1, /device:TPU:0, one launch (start us, length us, event | category | flops | bytes accessed | tf_op | source)
XLA Modules:
  0.0 456.8 jit_solution(4045173567904288285)
XLA Ops:
  0.6 1.4 reduce.54
  3.2 7.1 %all-to-all-start = ((s32[16,1,2]{2,1,0:T(1,128)}), s32[16,1,2]{2,1,0:T(1,128)S(1)}, u32[]{:S(2)}, u32[]{:S(2)}) async-start(s32[16,1,2]{2,1,0:T(1,128)} %bitcast), calls=%async_computation | async-start | bytes 16384 | tf_op jit(solution)/shard_map/all_to_all | solution.py:131
  11.4 6.4 %all-to-all-done = s32[16,1,2]{2,1,0:T(1,128)S(1)} async-done(((s32[16,1,2]{2,1,0:T(1,128)}), s32[16,1,2]{2,1,0:T(1,128)S(1)}, u32[]{:S(2)}, u32[]{:S(2)}) %all-to-all-start) | async-done | bytes 160 | tf_op jit(solution)/shard_map/all_to_all | solution.py:131
  17.8 17.9 %all_to_all.31 = f32[128,1,512]{2,1,0:T(1,128)S(1)} all-to-all(f32[128,1,512]{2,1,0:T(1,128)S(1)} %reshape.774), channel_id=1, replica_groups=mesh['row'=8,'col'=16] {'row','col'}, dimensions={0} | all-to-all | bytes 524288 | tf_op jit(solution)/shard_map/all_to_all | solution.py:15
  36.6 12.8 %all_to_all.32 = bf16[8,64,512]{2,1,0:T(8,128)(2,1)S(1)} all-to-all(bf16[8,64,512]{2,1,0:T(8,128)(2,1)S(1)} %broadcast_in_dim.16), channel_id=1, replica_groups=mesh['row'=8,'col'=16] {'row'}, dimensions={0} | all-to-all | bytes 1048576 | tf_op jit(solution)/shard_map/all_to_all | solution.py:35
  49.3 2.5 broadcast_in_dim.17
  51.8 3.7 all-to-all-start.4
  56.9 5.6 %convolution_convert_fusion = bf16[32,131072]{1,0:T(8,128)(2,1)} fusion(bf16[2,131072]{1,0:T(2,128)(2,1)S(1)} %reshape_reshape.6, s32[32]{0:T(128)S(1)} %compare_select_fusion.6), kind=kOutput, calls=%fused_computation.8 | convolution fusion | flops 20971584 | bytes 8913024 | tf_op jit(solution)/shard_map/dot_general | solution.py:152
  62.5 9.4 %reshape.631 = bf16[16,2,131072]{2,1,0:T(2,128)(2,1)} reshape(bf16[32,131072]{1,0:T(8,128)(2,1)} %convolution_convert_fusion) | data formatting | bytes 16777216 | tf_op jit(solution)/shard_map/reshape | solution.py:158
  71.8 13.9 %all-to-all-done.4 = bf16[16,2,64,512]{3,2,1,0:T(8,128)(2,1)S(1)} async-done(((bf16[16,2,64,512]{3,2,1,0:T(8,128)(2,1)}), bf16[16,2,64,512]{3,2,1,0:T(8,128)(2,1)S(1)}, u32[]{:S(2)}, u32[]{:S(2)}) %all-to-all-start.4) | async-done | bytes 2097184 | tf_op jit(solution)/shard_map/all_to_all | solution.py:35
  85.8 1.4 copy-done.3
  87.1 5.3 %all-to-all-start.2 = ((bf16[16,2,131072]{2,1,0:T(2,128)(2,1)}), bf16[16,2,131072]{2,1,0:T(2,128)(2,1)}, u32[]{:S(2)}, u32[]{:S(2)}) async-start(bf16[16,2,131072]{2,1,0:T(2,128)(2,1)} %reshape.631), calls=%async_computation.2 | async-start | bytes 16777216 | tf_op jit(solution)/shard_map/all_to_all | solution.py:160
  93.0 1.3 reduce.56
  94.4 2.7 copy.26
  97.2 8.9 %slice_reduce_fusion.19 = (f32[8192]{0:T(1024)S(1)}, f32[8192]{0:T(1024)S(1)}, f32[8192,1]{1,0:T(8,128)}, f32[8192,1]{1,0:T(8,128)}) fusion(f32[8192,8]{1,0:T(8,128)} %bitcast.99), kind=kLoop, calls=%fused_computation.112 | loop fusion | bytes 196608 | tf_op jit(solution)/shard_map/slice | solution.py:21
  106.1 11.8 %gather_fusion.4 = f32[2048]{0:T(1024)S(1)} fusion(f32[8192]{0:T(1024)S(1)} %get-tuple-element.6, s32[2048]{0:T(1024)S(1)} %fusion.27), kind=kCustom, calls=%fused_computation.3.clone | custom fusion | bytes 24576 | tf_op jit(solution)/shard_map/jit(_take)/gather | solution.py:180
  117.8 11.8 %gather_fusion = f32[2048]{0:T(1024)S(1)} fusion(f32[8192]{0:T(1024)S(1)} %get-tuple-element.6, s32[2048]{0:T(1024)S(1)} %fusion.26), kind=kCustom, calls=%fused_computation.clone | custom fusion | bytes 24576 | tf_op jit(solution)/shard_map/jit(_take)/gather | solution.py:180
  129.6 11.8 %gather_fusion.6 = f32[2048]{0:T(1024)S(1)} fusion(f32[8192]{0:T(1024)S(1)} %get-tuple-element.8, s32[2048]{0:T(1024)S(1)} %fusion.27), kind=kCustom, calls=%fused_computation.4.clone | custom fusion | bytes 24576 | tf_op jit(solution)/shard_map/jit(_take)/gather | solution.py:182
  141.4 11.8 %gather_fusion.2 = f32[2048]{0:T(1024)S(1)} fusion(f32[8192]{0:T(1024)S(1)} %get-tuple-element.8, s32[2048]{0:T(1024)S(1)} %fusion.26), kind=kCustom, calls=%fused_computation.2.clone | custom fusion | bytes 24576 | tf_op jit(solution)/shard_map/jit(_take)/gather | solution.py:182
  153.2 10.6 %slice_bitcast_fusion.3 = (f32[3,8192]{0,1:T(8,128)}, f32[3,8192]{0,1:T(8,128)}, f32[8192,3]{1,0:T(8,128)}, f32[8192,3]{1,0:T(8,128)}) fusion(f32[8192,8]{1,0:T(8,128)} %bitcast.100), kind=kLoop, calls=%fused_computation.111 | loop fusion | bytes 589824 | tf_op jit(solution)/shard_map/transpose | solution.py:22
  163.8 7.6 %gather_fusion.5 = f32[2048,3]{1,0:T(8,128)S(1)} fusion(f32[3,8192]{0,1:T(8,128)} %get-tuple-element.33, s32[2048]{0:T(1024)S(1)} %fusion.27), kind=kCustom, calls=%fused_computation.6.clone | custom fusion | bytes 57344 | tf_op jit(solution)/shard_map/jit(_take)/gather | solution.py:179
  171.4 7.6 %gather_fusion.1 = f32[2048,3]{1,0:T(8,128)S(1)} fusion(f32[3,8192]{0,1:T(8,128)} %get-tuple-element.33, s32[2048]{0:T(1024)S(1)} %fusion.26), kind=kCustom, calls=%fused_computation.1.clone | custom fusion | bytes 57344 | tf_op jit(solution)/shard_map/jit(_take)/gather | solution.py:179
  179.1 9.7 %gather_fusion.3 = f32[2048,3]{1,0:T(8,128)} fusion(f32[3,8192]{0,1:T(8,128)} %get-tuple-element.34, s32[2048]{0:T(1024)S(1)} %fusion.26), kind=kCustom, calls=%fused_computation.5.clone | custom fusion | bytes 57344 | tf_op jit(solution)/shard_map/jit(_take)/gather | solution.py:181
  188.8 9.9 %gather_fusion.7 = f32[2048,3]{1,0:T(8,128)} fusion(f32[3,8192]{0,1:T(8,128)} %get-tuple-element.34, s32[2048]{0:T(1024)S(1)} %fusion.27), kind=kCustom, calls=%fused_computation.7.clone | custom fusion | bytes 57344 | tf_op jit(solution)/shard_map/jit(_take)/gather | solution.py:181
  198.7 1.5 dynamic-slice_reduce_fusion
  200.4 1.3 dynamic-slice_bitcast_fusion
  203.3 1.6 select_bitcast_fusion.3
  204.8 1.4 slice_reduce_fusion.11
  206.3 1.6 select_bitcast_fusion.1
  207.9 1.4 slice_reduce_fusion.5
  209.4 1.4 slice_reduce_fusion.2
  210.9 1.4 slice_reduce_fusion.8
  212.4 33.1 %fusion.5 = (f32[1024,4,256]{0,2,1:T(8,128)}, f32[1024,4,256]{0,2,1:T(8,128)}) fusion(f32[1024]{0:T(1024)S(1)} %bitcast.118, f32[1024]{0:T(1024)S(1)} %bitcast.121, f32[1024]{0:T(1024)S(1)} %bitcast.115, f32[4,256]{1,0:T(4,128)S(1)} %mul.505, f32[4,256]{1,0:T(4,128)S(1)} %mul.502, f32[4,256]{1,0:T(4,128)S(1)} %mul.499, f32[4,256]{1,0:T(4,128)S(1)} %add.256, ...), kind=kLoop, calls=%fused_computation.25 | loop fusion | flops 37748736 | bytes 8445952 | tf_op jit(solution)/shard_map/convert_element_type | solution.py:80
  245.4 1.6 copy.27
  247.1 8.6 %reshape.632 = bf16[32,131072]{1,0:T(8,128)(2,1)} reshape(bf16[16,2,131072]{2,1,0:T(2,128)(2,1)} %all-to-all-done.2) | data formatting | bytes 16777216 | tf_op jit(solution)/shard_map/reshape | solution.py:163
  255.7 4.7 %convolution_convert_fusion.1 = bf16[16,131072]{1,0:T(8,128)(2,1)S(1)} fusion(bf16[32,131072]{1,0:T(8,128)(2,1)} %reshape.632, s32[16]{0:T(128)S(1)} %get-tuple-element.56), kind=kOutput, calls=%fused_computation.9 | convolution fusion | flops 136315392 | bytes 12582976 | tf_op jit(solution)/shard_map/dot_general | solution.py:161
  260.4 1.6 fusion.33
  262.0 2.2 reshape.733
  264.3 2.5 reshape.732
  266.8 3.0 fusion.13
  269.9 1.3 fusion.16
  272.1 33.9 %fusion.2 = f32[1024,512]{0,1:T(8,128)S(1)} fusion(f32[1024,4,256]{0,2,1:T(8,128)S(1)} %copy-done, bf16[4,512,512]{1,2,0:T(8,128)(2,1)S(1)} %bitcast.107, f32[4,512]{1,0:T(4,128)S(1)} %mul.529, f32[4,512]{1,0:T(4,128)S(1)} %mul.526, f32[4,512]{1,0:T(4,128)S(1)} %mul.523, f32[4,512]{1,0:T(4,128)S(1)} %add.263, f32[4,512]{1,0:T(4,128)S(1)} %sub.262, ...), kind=kOutput, calls=%fused_computation.16 | convolution fusion | flops 2186805248 | bytes 8466432 | tf_op jit(solution)/shard_map/gax,axy->gay/dot_general | solution.py:76
  306.1 33.6 %fusion = f32[1024,512]{0,1:T(8,128)S(1)} fusion(f32[1024,4,256]{0,2,1:T(8,128)S(1)} %copy-done.1, bf16[4,512,512]{1,2,0:T(8,128)(2,1)S(1)} %bitcast.106, f32[4,512]{1,0:T(4,128)S(1)} %mul.484, f32[4,512]{1,0:T(4,128)S(1)} %mul.481, f32[4,512]{1,0:T(4,128)S(1)} %mul.478, f32[4,512]{1,0:T(4,128)S(1)} %add.248, f32[4,512]{1,0:T(4,128)S(1)} %sub.235, ...), kind=kOutput, calls=%fused_computation.14 | convolution fusion | flops 2186805248 | bytes 8466432 | tf_op jit(solution)/shard_map/gax,axy->gay/dot_general | solution.py:76
  340.1 1.6 fusion.1
  341.7 33.7 %convolution_convert_fusion.3 = bf16[4,512,512]{1,2,0:T(8,128)(2,1)S(1)} fusion(bf16[1024,4,512]{0,2,1:T(8,128)(2,1)S(1)} %fusion.1, f32[4,512]{1,0:T(4,128)S(1)} %mul.484, f32[4,512]{1,0:T(4,128)S(1)} %mul.481, f32[4,512]{1,0:T(4,128)S(1)} %mul.478, f32[4,512]{1,0:T(4,128)S(1)} %add.248, f32[4,512]{1,0:T(4,128)S(1)} %sub.235, f32[1024]{0:T(1024)S(1)} %bitcast.126, ...), kind=kOutput, calls=%fused_computation.38 | convolution fusion | flops 2184183808 | bytes 6369280 | tf_op jit(solution)/shard_map/gax,gay->axy/dot_general | solution.py:89
  376.9 1.6 fusion.3
  378.5 42.9 %convolution_convert_fusion.2 = bf16[4,512,512]{1,2,0:T(8,128)(2,1)S(1)} fusion(bf16[1024,4,512]{0,2,1:T(8,128)(2,1)S(1)} %fusion.3, f32[4,512]{1,0:T(4,128)S(1)} %mul.529, f32[4,512]{1,0:T(4,128)S(1)} %mul.526, f32[4,512]{1,0:T(4,128)S(1)} %mul.523, f32[4,512]{1,0:T(4,128)S(1)} %add.263, f32[4,512]{1,0:T(4,128)S(1)} %sub.262, f32[1024]{0:T(1024)S(1)} %bitcast.120, ...), kind=kOutput, calls=%fused_computation.37 | convolution fusion | flops 2184183808 | bytes 6369280 | tf_op jit(solution)/shard_map/gax,gay->axy/dot_general | solution.py:89
  423.2 32.2 %all_to_all.33 = bf16[16,64,2,512]{3,1,2,0:T(8,128)(2,1)S(1)} all-to-all(bf16[16,64,2,512]{3,1,2,0:T(8,128)(2,1)S(1)} %copy.31), channel_id=1, replica_groups=mesh['row'=8,'col'=16] {'col'}, dimensions={0} | all-to-all | bytes 4194304 | tf_op jit(solution)/shard_map/all_to_all | solution.py:52
  (87 shorter events, 13.3 us)
Async XLA Ops:
  3.2 14.7 %all-to-all-start = ((s32[16,1,2]{2,1,0:T(1,128)}), s32[16,1,2]{2,1,0:T(1,128)S(1)}, u32[]{:S(2)}, u32[]{:S(2)}) async-start(s32[16,1,2]{2,1,0:T(1,128)} %bitcast), calls=%async_computation | async-start | bytes 16384 | tf_op jit(solution)/shard_map/all_to_all | solution.py:131
  51.8 33.9 %all-to-all-start.4 = ((bf16[16,2,64,512]{3,2,1,0:T(8,128)(2,1)}), bf16[16,2,64,512]{3,2,1,0:T(8,128)(2,1)S(1)}, u32[]{:S(2)}, u32[]{:S(2)}) async-start(bf16[16,2,64,512]{3,2,1,0:T(8,128)(2,1)} %broadcast_in_dim.17), calls=%async_computation.4 | async-start | bytes 4194304 | tf_op jit(solution)/shard_map/all_to_all | solution.py:35
  71.8 20.6 %copy-start.7 = (f32[2,1024]{1,0:T(2,128)S(1)}, f32[2,1024]{1,0:T(2,128)}, u32[]{:S(2)}) copy-start(f32[2,1024]{1,0:T(2,128)} %param.21) | copy-start | bytes 24580
  71.8 20.6 %copy-start.8 = (f32[2,1024]{1,0:T(2,128)S(1)}, f32[2,1024]{1,0:T(2,128)}, u32[]{:S(2)}) copy-start(f32[2,1024]{1,0:T(2,128)} %param.22) | copy-start | bytes 24580
  71.8 20.7 %copy-start.6 = (f32[2,3,1024]{2,0,1:T(2,128)S(1)}, f32[2,3,1024]{2,0,1:T(2,128)}, u32[]{:S(2)}) copy-start(f32[2,3,1024]{2,0,1:T(2,128)} %param.20) | copy-start | bytes 73732
  85.8 1.4 copy-start.3
  87.1 159.9 %all-to-all-start.2 = ((bf16[16,2,131072]{2,1,0:T(2,128)(2,1)}), bf16[16,2,131072]{2,1,0:T(2,128)(2,1)}, u32[]{:S(2)}, u32[]{:S(2)}) async-start(bf16[16,2,131072]{2,1,0:T(2,128)(2,1)} %reshape.631), calls=%async_computation.2 | async-start | bytes 16777216 | tf_op jit(solution)/shard_map/all_to_all | solution.py:160
  212.3 33.1 %copy-start.4 = (bf16[16,2,64,512]{3,2,1,0:T(8,128)(2,1)S(1)}, bf16[16,2,64,512]{3,2,1,0:T(8,128)(2,1)}, u32[]{:S(2)}) copy-start(bf16[16,2,64,512]{3,2,1,0:T(8,128)(2,1)} %copy-done.3) | copy-start | bytes 6291460
  266.8 3.1 copy-start.2
  266.8 3.1 copy-start.5
  269.9 2.2 copy-start
  272.1 34.0 %copy-start.1 = (f32[1024,4,256]{0,2,1:T(8,128)S(1)}, f32[1024,4,256]{0,2,1:T(8,128)}, u32[]{:S(2)}) copy-start(f32[1024,4,256]{0,2,1:T(8,128)} %get-tuple-element.40) | copy-start | bytes 12582916
